TPU v7x, 768 devices: a whole 4x8x12 slice. The times are simulated.
768 devices in a mesh: freq: 48 (over y_lo, z), cell: 16 (over x, y_hi, core).
Axes of the slice: x: 4, y: 8 (y_hi: 2, y_lo: 4; y = y_hi * 4 + y_lo), z: 12, core: 2. Of those that a mesh axis runs over, the one named last changes fastest.
Arguments:
- columns: float32 [2, 96, 384, 600], P(None, 'freq'), may hold values from -6 to 6
- freq_blocks: float32 [2, 96, 600, 4096], P(None, 'freq', None, 'cell'), may hold values from -0.09375 to 0.09375
- causal_cutoffs: int32 [384], replicated, may hold values from 23 to 95
- band_index: int32 [4096], P('cell'), may hold values from 0 to 7
- band_rates: float32 [8], replicated, may hold values from 0.05 to 0.45
Outputs:
- hessian_columns: float32 [2, 96, 384, 600], P(None, 'freq', 'cell')
All inputs are finite; a program needn't handle non-finite values.
Results may differ from a plain program's by a relative error of at most 0.00007.
Values sent between devices are 32-bit elements; how exact they have to be, the bound alone decides.
A program may use at most 64 MiB of HBM per device.

v0:
```python
import math

import jax
import jax.numpy as jnp
from jax import lax
from jax.sharding import Mesh
from jax.sharding import PartitionSpec as P

MODE_SHARE_WIDTH = 8
C_DEV = 256
SWEEPS = 4
BANDS = 8
CELL = ("cell_0", "cell_1", "cell_2")


precise = lax.Precision.HIGHEST


def extended(shard, sides, width):
    for axis, dim in sides:
        devices, length = (lax.axis_size(axis), shard.shape[dim])
        up = [(i, (i + 1) % devices) for i in range(devices - 1)]
        down = [(j, i) for i, j in up]
        last = lax.slice_in_dim(shard, length - width, length, axis=dim)
        leading = lax.slice_in_dim(shard, 0, width, axis=dim)
        before = lax.ppermute(last, axis, up)
        after = lax.ppermute(leading, axis, down)
        shard = jnp.concatenate([before, shard, after], axis=dim)
    return shard


def split_up(shard, dim, devices):
    before, after = (shard.shape[:dim], shard.shape[dim + 1 :])
    return jnp.moveaxis(shard.reshape(*before, devices, -1, *after), dim, 0)


def summed_rows(shard, chips, core, dim):
    sizes = (lax.axis_size(chips), lax.axis_size(core))
    parts = split_up(shard, dim, sizes[0] * sizes[1])
    inside = parts.shape[1:]
    parts = parts.reshape(*sizes, *inside).swapaxes(0, 1).reshape(-1, *inside)
    parts = lax.psum_scatter(parts, core, scatter_dimension=0, tiled=True)
    return lax.psum_scatter(parts, chips, scatter_dimension=0, tiled=True)[0]


def inverse_table(epoch_number, harmonic_number):
    cycle_length = 2 * epoch_number
    sample_moments = lax.broadcasted_iota(jnp.int32, (epoch_number, harmonic_number), 0)
    harmonic_rate = lax.broadcasted_iota(jnp.int32, (epoch_number, harmonic_number), 1)
    harmonic_offsets = (sample_moments * harmonic_rate % cycle_length).astype(jnp.float32) * (
        2.0 * math.pi / cycle_length
    )
    weight = (
        jnp.where((harmonic_rate == 0) | (harmonic_rate == harmonic_number - 1), 1.0, 2.0).astype(
            jnp.float32
        )
        / cycle_length
    )
    return jnp.concatenate(
        [weight * jnp.cos(harmonic_offsets), -weight * jnp.sin(harmonic_offsets)], axis=1
    )


def forward_table(epoch_number, harmonic_number):
    cycle_length = 2 * epoch_number
    harmonic_rate = lax.broadcasted_iota(jnp.int32, (harmonic_number, epoch_number), 0)
    sample_moments = lax.broadcasted_iota(jnp.int32, (harmonic_number, epoch_number), 1)
    harmonic_offsets = (sample_moments * harmonic_rate % cycle_length).astype(jnp.float32) * (
        2.0 * math.pi / cycle_length
    )
    return jnp.concatenate([jnp.cos(harmonic_offsets), -jnp.sin(harmonic_offsets)], axis=0)


def adjoint_product(columns, blocks):
    real_part = jnp.einsum("kjs,ksm->kjm", columns[0], blocks[0], precision=precise) + jnp.einsum(
        "kjs,ksm->kjm", columns[1], blocks[1], precision=precise
    )
    imag_part = jnp.einsum("kjs,ksm->kjm", columns[1], blocks[0], precision=precise) - jnp.einsum(
        "kjs,ksm->kjm", columns[0], blocks[1], precision=precise
    )
    return jnp.stack([real_part, imag_part])


def forward_product(spectrum, blocks):
    real_part = jnp.einsum("kjm,ksm->kjs", spectrum[0], blocks[0], precision=precise) - jnp.einsum(
        "kjm,ksm->kjs", spectrum[1], blocks[1], precision=precise
    )
    imag_part = jnp.einsum("kjm,ksm->kjs", spectrum[1], blocks[0], precision=precise) + jnp.einsum(
        "kjm,ksm->kjs", spectrum[0], blocks[1], precision=precise
    )
    return jnp.stack([real_part, imag_part])


def on_device(columns, freq_blocks, causal_cutoffs, band_index, band_rates):
    local_spectrum = adjoint_product(columns, freq_blocks)
    gathered = lax.all_to_all(local_spectrum, "freq", split_axis=2, concat_axis=1, tiled=True)
    freq_total = gathered.shape[1]
    horizon_span = freq_total - 1
    sampled_trace = jnp.dot(
        inverse_table(horizon_span, freq_total),
        gathered.reshape(2 * freq_total, MODE_SHARE_WIDTH * C_DEV),
        precision=precise,
        preferred_element_type=jnp.float32,
    )
    sampled_trace = sampled_trace.reshape(horizon_span, MODE_SHARE_WIDTH, C_DEV)
    device_ranges = lax.dynamic_slice_in_dim(
        causal_cutoffs, lax.axis_index("freq") * MODE_SHARE_WIDTH, MODE_SHARE_WIDTH
    )
    sample_moments = lax.broadcasted_iota(jnp.int32, (horizon_span, MODE_SHARE_WIDTH), 0)
    sampled_trace = jnp.where(
        (sample_moments < device_ranges[None, :])[:, :, None], sampled_trace, 0.0
    )
    flat = sampled_trace.reshape(horizon_span * MODE_SHARE_WIDTH, C_DEV)
    levels = lax.broadcasted_iota(jnp.int32, (BANDS, C_DEV), 0)
    cell_rates = jnp.sum(jnp.where(levels == band_index[None, :], band_rates[:, None], 0.0), axis=0)
    stacked = jnp.concatenate([flat, cell_rates[None, :]], axis=0)
    padded = extended(stacked, ((CELL, 1),), SWEEPS)
    field = padded[:-1]
    margin_rates = padded[-1]
    for repeat in range(SWEEPS):
        inner_rates = margin_rates[1:-1]
        field = field[:, 1:-1] + inner_rates * (field[:, :-2] - 2.0 * field[:, 1:-1] + field[:, 2:])
        margin_rates = inner_rates
    flat = field
    spectrum = jnp.dot(
        forward_table(horizon_span, freq_total),
        flat.reshape(horizon_span, MODE_SHARE_WIDTH * C_DEV),
        precision=precise,
        preferred_element_type=jnp.float32,
    )
    spectrum = spectrum.reshape(2, freq_total, MODE_SHARE_WIDTH, C_DEV)
    returned = lax.all_to_all(spectrum, "freq", split_axis=1, concat_axis=2, tiled=True)
    partial_terms = forward_product(returned, freq_blocks)
    return summed_rows(partial_terms, ("cell_0", "cell_1"), "cell_2", 2)


def solution(mesh):
    torus = Mesh(
        mesh.devices.reshape(mesh.shape["freq"], 4, 2, 2), ("freq", "cell_0", "cell_1", "cell_2")
    )
    placed = (P(None, "freq", None, None), P(None, "freq", None, CELL), P(), P(CELL), P())
    return jax.shard_map(
        on_device,
        mesh=torus,
        in_specs=placed,
        out_specs=P(None, "freq", CELL, None),
        check_vma=False,
    )
```

profile of v0, /device:TPU:1, one launch (start us, length us, event | category | flops | bytes accessed | tf_op | source)
XLA Modules:
  0.0 362.7 jit_solution(8512012555034039679)
XLA Ops:
  6.5 5.3 %fusion = f32[2,384,256]{2,1,0:T(8,128)S(1)} fusion(f32[2,2,384,600]{2,3,1,0:T(8,128)} %param.5, f32[2,2,600,256]{3,2,1,0:T(8,128)} %param.6), kind=kOutput, calls=%fused_computation.1 | convolution fusion | flops 1415577600 | bytes 3858432 | tf_op jit(solution)/shard_map/kjs,ksm->kjm/dot_general | solution.py:78
  11.9 5.0 %fusion.2 = f32[2,384,256]{2,1,0:T(8,128)S(1)} fusion(f32[2,2,384,600]{2,3,1,0:T(8,128)} %param.5, f32[2,2,600,256]{3,2,1,0:T(8,128)S(1)} %copy-done), kind=kOutput, calls=%fused_computation.3 | convolution fusion | flops 1415577600 | bytes 3858432 | tf_op jit(solution)/shard_map/kjs,ksm->kjm/dot_general | solution.py:75
  16.8 3.4 fusion.27
  20.3 3.6 fusion.21
  23.9 2.4 copy.28
  26.3 19.7 %all-to-all-start = ((f32[2,2,384,256]{3,1,0,2:T(2,128)}), f32[2,2,384,256]{3,1,0,2:T(2,128)}, u32[]{:S(2)}, u32[]{:S(2)}) async-start(f32[2,2,384,256]{3,1,0,2:T(2,128)} %copy.28), calls=%async_computation | async-start | bytes 3145728 | tf_op jit(solution)/shard_map/all_to_all | solution.py:96
  46.1 0.8 dynamic_slice.3
  47.5 51.1 %all-to-all-done = f32[2,2,384,256]{3,1,0,2:T(2,128)} async-done(((f32[2,2,384,256]{3,1,0,2:T(2,128)}), f32[2,2,384,256]{3,1,0,2:T(2,128)}, u32[]{:S(2)}, u32[]{:S(2)}) %all-to-all-start) | async-done | bytes 1572896 | tf_op jit(solution)/shard_map/all_to_all | solution.py:96
  98.6 1.7 copy.29
  100.3 1.4 fusion.15
  102.4 10.2 %collective-permute-start = (f32[761,4]{1,0:T(8,128)S(1)}, f32[761,4]{1,0:T(8,128)S(1)}, u32[]{:S(2)}, u32[]{:S(2)}) collective-permute-start(f32[761,4]{1,0:T(8,128)S(1)} %get-tuple-element.5), channel_id=1, source_target_pairs={{0,1},{1,2},{2,3},{3,4},{4,5},{5,6},{6,7},{7,8},{8,9},{9,10},{10,1... | collective-permute-start | bytes 36536 | tf_op jit(solution)/shard_map/ppermute | solution.py:26
  112.6 1.9 collective-permute-start.1
  114.5 2.8 collective-permute-done
  117.3 12.5 %collective-permute-done.1 = f32[761,4]{1,0:T(8,128)S(1)} collective-permute-done((f32[761,4]{1,0:T(8,128)S(1)}, f32[761,4]{1,0:T(8,128)S(1)}, u32[]{:S(2)}, u32[]{:S(2)}) %collective-permute-start.1) | collective-permute-done | bytes 12208 | tf_op jit(solution)/shard_map/ppermute | solution.py:27
  130.4 0.7 fusion.45
  131.1 0.7 fusion.43
  131.9 0.7 fusion.41
  132.6 1.4 fusion.58
  133.9 1.2 reshape.58
  135.5 1.6 fusion.54
  137.1 0.9 copy.33
  138.0 53.9 %all_to_all.30 = f32[2,96,8,256]{3,2,0,1:T(8,128)S(1)} all-to-all(f32[2,96,8,256]{3,2,0,1:T(8,128)S(1)} %copy.33), channel_id=1, replica_groups=mesh['freq'=48,'cell_0'=4,'cell_1'=2,'cell_2'=2] {'freq'}, dimensions={1} | all-to-all | bytes 3145728 | tf_op jit(solution)/shard_map/all_to_all | solution.py:132
  192.1 2.2 fusion.34
  194.2 3.4 fusion.36
  197.6 3.4 convolution_add_fusion
  201.0 2.8 copy.36
  203.9 5.1 %convolution_subtract_fusion = f32[2,384,600]{1,2,0:T(8,128)} fusion(f32[2,384,600]{1,2,0:T(8,128)} %fusion.36, f32[2,2,600,256]{3,2,1,0:T(8,128)S(1)} %copy-done, f32[2,2,48,8,256]{4,3,2,1,0:T(8,128)} %bitcast.110), kind=kOutput, calls=%fused_computation.19 | convolution fusion | flops 1416038400 | bytes 5701632 | tf_op jit(solution)/shard_map/kjm,ksm->kjs/dot_general | solution.py:85
  209.0 3.0 copy.35
  212.0 1.8 pad_maximum_fusion
  213.8 2.3 copy.37
  216.2 31.1 %reduce-scatter.3.cloned.1.call-done = f32[8,2,2,24,600]{4,3,2,1,0:T(8,128)} async-done(((f32[16,2,2,24,600]{4,3,2,1,0:T(8,128)}), f32[8,2,2,24,600]{4,3,2,1,0:T(8,128)}) %reduce-scatter.3.cloned.1.call-update) | async-done | bytes 1843216 | tf_op jit(solution)/shard_map/reduce_scatter | solution.py:42
  247.3 108.5 %reduce-scatter.5.cloned.1.call-done = f32[1,2,2,24,600]{4,3,2,1,0:T(8,128)} async-done(((f32[8,2,2,24,600]{4,3,2,1,0:T(8,128)}), f32[1,2,2,24,600]{4,3,2,1,0:T(8,128)}) %reduce-scatter.5.cloned.1.call-update) | async-done | bytes 230416 | tf_op jit(solution)/shard_map/reduce_scatter | solution.py:43
  (33 shorter events, 2.6 us)
Async XLA Ops:
  6.5 5.3 %copy-start = (f32[2,2,600,256]{3,2,1,0:T(8,128)S(1)}, f32[2,2,600,256]{3,2,1,0:T(8,128)}, u32[]{:S(2)}) copy-start(f32[2,2,600,256]{3,2,1,0:T(8,128)} %param.6) | copy-start | bytes 7372804
  11.9 5.0 %copy-start.1 = (f32[2,2,384,600]{2,3,1,0:T(8,128)S(1)}, f32[2,2,384,600]{2,3,1,0:T(8,128)}, u32[]{:S(2)}) copy-start(f32[2,2,384,600]{2,3,1,0:T(8,128)} %param.5) | copy-start | bytes 11059204
  26.3 20.6 %copy-start.4 = (s32[256]{0:T(256)S(1)}, s32[256]{0:T(256)}, u32[]{:S(2)}) copy-start(s32[256]{0:T(256)} %param.8) | copy-start | bytes 3076
  26.3 20.6 %copy-start.5 = (f32[8]{0:T(128)S(1)}, f32[8]{0:T(128)}, u32[]{:S(2)}) copy-start(f32[8]{0:T(128)} %param.9) | copy-start | bytes 100
  26.3 72.3 %all-to-all-start = ((f32[2,2,384,256]{3,1,0,2:T(2,128)}), f32[2,2,384,256]{3,1,0,2:T(2,128)}, u32[]{:S(2)}, u32[]{:S(2)}) async-start(f32[2,2,384,256]{3,1,0,2:T(2,128)} %copy.28), calls=%async_computation | async-start | bytes 3145728 | tf_op jit(solution)/shard_map/all_to_all | solution.py:96
  46.0 201.3 %reduce-scatter.3.cloned.1.call-start = ((), (), s32[]{:S(2)}) async-start(), calls=%async_computation.4 | async-start | bytes 5898240 | tf_op jit(solution)/shard_map/reduce_scatter | solution.py:42
  102.4 14.9 %collective-permute-start = (f32[761,4]{1,0:T(8,128)S(1)}, f32[761,4]{1,0:T(8,128)S(1)}, u32[]{:S(2)}, u32[]{:S(2)}) collective-permute-start(f32[761,4]{1,0:T(8,128)S(1)} %get-tuple-element.5), channel_id=1, source_target_pairs={{0,1},{1,2},{2,3},{3,4},{4,5},{5,6},{6,7},{7,8},{8,9},{9,10},{10,1... | collective-permute-start | bytes 36536 | tf_op jit(solution)/shard_map/ppermute | solution.py:26
  112.6 17.2 %collective-permute-start.1 = (f32[761,4]{1,0:T(8,128)S(1)}, f32[761,4]{1,0:T(8,128)S(1)}, u32[]{:S(2)}, u32[]{:S(2)}) collective-permute-start(f32[761,4]{1,0:T(8,128)S(1)} %get-tuple-element.6), channel_id=1, source_target_pairs={{1,0},{2,1},{3,2},{4,3},{5,4},{6,5},{7,6},{8,7},{9,8},{10,9},{11,1... | collective-permute-start | bytes 36536 | tf_op jit(solution)/shard_map/ppermute | solution.py:27
  192.1 5.5 %copy-start.2 = (f32[2,48,2,8,256]{4,3,1,2,0:T(8,128)}, f32[2,48,2,8,256]{4,3,1,2,0:T(8,128)S(1)}, u32[]{:S(2)}) copy-start(f32[2,48,2,8,256]{4,3,1,2,0:T(8,128)S(1)} %copy.57) | copy-start | bytes 4718596
  209.0 3.0 copy-start.3
  216.1 139.7 %reduce-scatter.5.cloned.1.call-start = ((), (), s32[]{:S(2)}) async-start(), calls=%async_computation.5 | async-start | bytes 2211840 | tf_op jit(solution)/shard_map/reduce_scatter | solution.py:43
Sparse Core Ops, SparseCore 0:
  216.2 31.0 reduce-scatter.2
  252.6 103.2 reduce-scatter.4
where the time goes:
time: 364 us; the launch traced here: 363 us
  waiting for transfers between devices  206 us (57%)
  blocking collectives  53.9 us (15%)
  matrix products  34.3 us (9%)
  starting transfers between devices  31.9 us (9%)
  local copies, waits for them, and re-layouts  16 us (4%)
  between operations  13.7 us (4%)
  other arithmetic  6.8 us (2%)
    reduce_scatter x1, waiting for transfers between devices, summed_rows(): return lax.psum_scatter(parts, chips, scatter_dimension=0, tiled=True)[0]  109 us
    all_to_all x1, blocking collectives, on_device(): lax.all_to_all(spectrum, 'freq', split_axis=1, concat_axis=2, tiled=True)  53.9 us
    all_to_all x1, waiting for transfers between devices, on_device(): lax.all_to_all(local_spectrum, 'freq', split_axis=2, concat_axis=1, tiled...  51.1 us
    reduce_scatter x1, waiting for transfers between devices, summed_rows(): parts = lax.psum_scatter(parts, core, scatter_dimension=0, tiled=True)  31.1 us
    all_to_all x1, starting transfers between devices, on_device(): lax.all_to_all(local_spectrum, 'freq', split_axis=2, concat_axis=1, tiled...  19.7 us
    ppermute x1, waiting for transfers between devices, extended(): after = lax.ppermute(leading, axis, down)  12.5 us
    ppermute x1, starting transfers between devices, extended(): before = lax.ppermute(last, axis, up)  10.2 us
  transfers between devices with their start and end apart: 5, of which 5 were waited for; matrix products, arithmetic and copies ran while one was open for 0% of the time, Pallas kernels for 0%

commit v1 on v0

v1 whole, which is shorter than its diff:
```python
import math

import jax
import jax.numpy as jnp
import numpy as np
from jax import lax
from jax.experimental import pallas as pl
from jax.experimental.pallas import tpu as pltpu
from jax.sharding import Mesh
from jax.sharding import PartitionSpec as P

AXES = ("ylo", "z", "x", "yhi", "core")
YLO, ZED, EX, YHI, CORES = 4, 12, 4, 2, 2
FREQ_DEVICES = YLO * ZED
NF = 96
NT = 95
TP = 96
NS = 600
NSP = 640
NJ = 384
JD = 8
CD = 256
SWEEPS = 4
BANDS = 8
OUT_COLS = 24
MESH = pl.DeviceIdType.MESH
F32, BF16 = jnp.float32, jnp.bfloat16


def halves(table):
    high = table.astype(np.float32).astype(jnp.bfloat16)
    low = (table - high.astype(np.float64)).astype(jnp.bfloat16)
    return high, low


def tables():
    cycle = 2 * NT
    k = np.arange(NF)
    t = np.arange(NT)
    angle = 2.0 * math.pi * ((t[:, None] * k[None, :]) % cycle) / cycle
    weight = np.where((k == 0) | (k == NF - 1), 1.0, 2.0) / cycle
    inv = np.stack([weight * np.cos(angle), -weight * np.sin(angle)], axis=-1)
    inv = inv.reshape(NT, FREQ_DEVICES, 2, 2).transpose(0, 2, 1, 3).reshape(NT, 2 * NF)
    inv = np.concatenate([inv, np.zeros((TP - NT, 2 * NF))], axis=0)
    fwd = np.stack([np.cos(angle), -np.sin(angle)], axis=-1)
    fwd = fwd.reshape(NT, FREQ_DEVICES, 2, 2).transpose(2, 1, 3, 0).reshape(2, NF, NT)
    fwd = np.concatenate([fwd, np.zeros((2, NF, TP - NT))], axis=2)
    return (
        np.concatenate(halves(inv), axis=0),
        np.concatenate(halves(fwd), axis=1),
    )


def split(x):
    high = x.astype(BF16)
    return high, (x - high.astype(F32)).astype(BF16)


def mm(a, b):
    return lax.dot_general(a, b, (((1,), (0,)), ((), ())), preferred_element_type=F32)


def mt(a, b):
    return lax.dot_general(a, b, (((1,), (1,)), ((), ())), preferred_element_type=F32)


def kernel(
    cut_ref, rates_ref, cols_ref, blocks_ref, bands_ref, inv_ref, fwd_ref, out_ref,
    cols, blocks, vh, vl, gh, gl, adj, got1, ext, uh, ul, rate, pack, halo, send2, got2,
    part, r1, r2a, r2b, r3,
    load_sem, self_sem, send_sem1, recv_sem1, send_sem2, recv_sem2, hsend, hrecv, rsend, rrecv,
):
    y, z = lax.axis_index("ylo"), lax.axis_index("z")
    x, yhi, core = lax.axis_index("x"), lax.axis_index("yhi"), lax.axis_index("core")
    me = y * ZED + z
    cell = (x * YHI + yhi) * CORES + core
    swap = x + 1 - 2 * lax.rem(x, 2)
    flip = 3 - x
    flip_swap = flip + 1 - 2 * lax.rem(flip, 2)

    loads = []
    for k in range(2):
        loads.append(pltpu.make_async_copy(blocks_ref.at[:, k], blocks.at[k], load_sem.at[2 * k]))
        loads.append(pltpu.make_async_copy(cols_ref.at[:, k], cols.at[k], load_sem.at[2 * k + 1]))
    for copy in loads:
        copy.start()

    def peer(i):
        turn = lax.rem(i, 4)
        step = lax.div(i, 4)
        half = 5 - lax.div(step - 1, 2)
        up = lax.rem(step, 2) == 1
        dz = jnp.where(step == 0, 6, jnp.where(up, half, 12 - half))
        dz = jnp.where(step == 11, 0, dz)
        return lax.rem(y + 3 - turn, YLO), lax.rem(z + dz, ZED)

    def cell_peer(c):
        c = lax.rem(c + 16, 16)
        return {"x": lax.div(c, 4), "yhi": lax.rem(lax.div(c, 2), 2), "core": lax.rem(c, 2)}

    left, right = cell_peer(cell - 1), cell_peer(cell + 1)
    sibling, over = {"core": 1 - core}, {"yhi": 1 - yhi}

    barrier = pltpu.get_barrier_semaphore()

    def greet(i, carry):
        py, pz = peer(i)
        pl.semaphore_signal(barrier, inc=1, device_id={"ylo": py, "z": pz}, device_id_type=MESH)
        return carry

    lax.fori_loop(0, FREQ_DEVICES - 1, greet, 0)
    friends = [left, right, sibling, over, {"x": swap}, {"x": flip}]
    for friend in friends:
        pl.semaphore_signal(barrier, inc=1, device_id=friend, device_id_type=MESH)

    vh[...] = jnp.zeros_like(vh)
    vl[...] = jnp.zeros_like(vl)

    def operands(k):
        blank = jnp.zeros((NSP - NS, CD), F32)
        for part_index in range(2):
            value = jnp.concatenate([blocks[k, part_index], blank], axis=0)
            high, low = split(value)
            for into, half in ((gh, high), (gl, low)):
                if part_index == 0:
                    into[k, 0:NSP, 0:CD] = half
                    into[k, NSP:, CD:] = half
                else:
                    into[k, 0:NSP, CD:] = -half
                    into[k, NSP:, 0:CD] = half
            high, low = split(cols[k, part_index])
            vh[:, part_index * NSP : part_index * NSP + NS] = high
            vl[:, part_index * NSP : part_index * NSP + NS] = low

    def exchange(k, source, target, send_sem, recv_sem):
        def send(i, carry):
            py, pz = peer(i)
            dest = py * ZED + pz
            pltpu.make_async_remote_copy(
                src_ref=source(k, dest),
                dst_ref=target(k, me),
                send_sem=send_sem.at[k],
                recv_sem=recv_sem.at[k],
                device_id={"ylo": py, "z": pz},
                device_id_type=MESH,
            ).start()
            return carry

        lax.fori_loop(0, FREQ_DEVICES - 1, send, 0)

    adj_at = lambda k, f: adj.at[k, f]
    got1_at = lambda k, f: got1.at[k, :, pl.ds(pl.multiple_of(16 * f, 16), 16), :]
    send2_at = lambda k, f: send2.at[k, :, pl.ds(pl.multiple_of(16 * f, 16), 16), :]
    got2_at = lambda k, f: got2.at[k, f]

    own1, own2 = [], []
    for k in range(2):
        loads[2 * k].wait()
        loads[2 * k + 1].wait()
        operands(k)
        both = mm(vh[...], gh[k]) + mm(vh[...], gl[k]) + mm(vl[...], gh[k])
        for c in range(4):
            quarter = both[:, c * 128 : c * 128 + 128].reshape(FREQ_DEVICES, JD, 128)
            adj[k, :, c % 2, c // 2 * JD : c // 2 * JD + JD, :] = quarter
        if k == 0:
            pl.semaphore_wait(barrier, FREQ_DEVICES - 1 + len(friends))
        exchange(k, adj_at, got1_at, send_sem1, recv_sem1)
        own1.append(pltpu.make_async_copy(adj_at(k, me), got1_at(k, me), self_sem.at[k]))
        own1[k].start()

    band = bands_ref[...]
    own_rate = jnp.zeros((JD, CD), F32)
    for b in range(BANDS):
        own_rate = own_rate + jnp.where(band == b, rates_ref[b], 0.0)
    rate[:, 0:CD] = own_rate

    def all_but_one(buffer, k, send_sem, recv_sem):
        return pltpu.make_async_remote_copy(
            src_ref=buffer,
            dst_ref=buffer,
            send_sem=send_sem.at[k],
            recv_sem=recv_sem.at[k],
            device_id={"core": 1 - core},
            device_id_type=MESH,
        )

    for k in range(2):
        own1[k].wait()
        all_but_one(got1.at[k, :, pl.ds(0, 47 * 16), :], k, send_sem1, recv_sem1).wait_recv()

    time = lax.broadcasted_iota(jnp.int32, (TP, CD), 0)
    lane = lax.broadcasted_iota(jnp.int32, (TP // 4, 128), 1)
    to_left = jnp.zeros((TP // 4, 128), F32)
    to_right = jnp.zeros((TP // 4, 128), F32)
    for j in range(JD):
        value = jnp.concatenate(
            [
                jnp.concatenate([got1[k, h, pl.ds(j, NF, stride=JD), :] for h in range(2)], axis=1)
                for k in range(2)
            ],
            axis=0,
        )
        high, low = split(value)
        main = mm(inv_ref[...], high)
        series = main[0:TP] + main[TP:] + mm(inv_ref[0:TP], low)
        series = jnp.where(time < cut_ref[JD * me + j], series, 0.0)
        ext[j, :, 0:CD] = series
        for g in range(4):
            rows = slice(g * 24, g * 24 + 24)
            at = 32 * g + 4 * j
            here = (lane >= at) & (lane < at + 4)
            head, tail = series[rows, 0:128], series[rows, 128:256]
            head = pltpu.roll(head, at, 1) if at else head
            tail = pltpu.roll(tail, (at + 4) % 128, 1) if (at + 4) % 128 else tail
            to_left = jnp.where(here, head, to_left)
            to_right = jnp.where(here, tail, to_right)
    pack[0, 0:24] = to_left
    pack[1, 0:24] = to_right
    pack[0, 24:32] = own_rate[:, 0:128]
    pack[1, 24:32] = own_rate[:, 128:256]

    edge = []
    for side, friend in ((0, left), (1, right)):
        edge.append(
            pltpu.make_async_remote_copy(
                src_ref=pack.at[side],
                dst_ref=halo.at[side],
                send_sem=hsend.at[side],
                recv_sem=hrecv.at[side],
                device_id=friend,
                device_id_type=MESH,
            )
        )
        edge[side].start()
    for copy in edge:
        copy.wait()

    after = jnp.where(cell < 15, 1.0, 0.0)
    before = jnp.where(cell > 0, 1.0, 0.0)
    from_right, from_left = halo[0, 0:24] * after, halo[1, 0:24] * before
    lane8 = lax.broadcasted_iota(jnp.int32, (JD, 128), 1)
    far = jnp.where(lane8 < 4, halo[0, 24:32] * after, 0.0)
    far = jnp.where(lane8 >= 124, halo[1, 24:32] * before, far)
    rate[:, CD:] = far
    lane24 = lax.broadcasted_iota(jnp.int32, (TP // 4, 128), 1)

    for j in range(JD):
        for g in range(4):
            at = 32 * g + 4 * j
            first = pltpu.roll(from_right, 128 - at, 1) if at else from_right
            last = pltpu.roll(from_left, (252 - at) % 128, 1) if (252 - at) % 128 else from_left
            tile = jnp.where(lane24 < 4, first, jnp.where(lane24 >= 124, last, 0.0))
            ext[j, g * 24 : g * 24 + 24, CD:] = tile

    def smooth(j, carry):
        field = ext[j]
        rates = rate[0:1, :]
        for _ in range(SWEEPS):
            field = field + rates * (
                pltpu.roll(field, 1, 1) - 2.0 * field + pltpu.roll(field, CD + 127, 1)
            )
        high, low = split(field[:, 0:CD])
        uh[j] = high
        ul[j] = low
        return carry

    lax.fori_loop(0, JD, smooth, 0)

    for k in range(2):
        for j in range(JD):
            main = mm(fwd_ref[k], uh[j])
            main = main[0:NF] + main[NF:] + mm(fwd_ref[k, 0:NF], ul[j])
            for h in range(2):
                send2[k, h, pl.ds(j, NF, stride=JD), :] = main[:, h * 128 : h * 128 + 128]
        exchange(k, send2_at, got2_at, send_sem2, recv_sem2)
        own2.append(pltpu.make_async_copy(send2_at(k, me), got2_at(k, me), self_sem.at[2 + k]))
        own2[k].start()

    def move(k, i, source, target, friend):
        return pltpu.make_async_remote_copy(
            src_ref=source,
            dst_ref=target,
            send_sem=rsend.at[k, i],
            recv_sem=rrecv.at[k, i],
            device_id=friend,
            device_id_type=MESH,
        )

    for k in range(2):
        own2[k].wait()
        all_but_one(got2.at[k, pl.ds(0, 47)], k, send_sem2, recv_sem2).wait_recv()
        quarters = [
            split(got2[k, :, c % 2, c // 2 * JD : c // 2 * JD + JD, :].reshape(NJ, 128))
            for c in range(4)
        ]
        ch = jnp.concatenate([high for high, _ in quarters], axis=1)
        cl = jnp.concatenate([low for _, low in quarters], axis=1)
        for h in range(2):
            rows = slice(h * NSP, h * NSP + NSP)
            res = mt(ch, gh[k, rows, :]) + mt(ch, gl[k, rows, :]) + mt(cl, gh[k, rows, :])
            for c in range(16):
                part[k, c % 2, h, c // 4, (c // 2) % 2] = res[c * OUT_COLS : (c + 1) * OUT_COLS]
        mine = part.at[k, core]
        s1 = move(k, 0, part.at[k, 1 - core], r1.at[k], sibling)
        s1.start()
        s1.wait()
        part[k, core] = part[k, core] + r1[k]
        s2 = [
            move(k, 1, mine.at[0, swap], r2a.at[k, 0, 0], {"x": swap}),
            move(k, 2, mine.at[0, flip_swap], r2a.at[k, 0, 1], {"x": swap}),
            move(k, 3, mine.at[1, flip], r2a.at[k, 1, 0], {"x": flip}),
            move(k, 4, mine.at[1, flip_swap], r2a.at[k, 1, 1], {"x": flip}),
        ]
        for copy in s2:
            copy.start()
        for copy in s2:
            copy.wait()
        part[k, core, 0, flip] = part[k, core, 0, flip] + r2a[k, 0, 1]
        part[k, core, 1, swap] = part[k, core, 1, swap] + r2a[k, 1, 1]
        s3 = [
            move(k, 5, mine.at[0, flip], r2b.at[k, 0], {"x": flip}),
            move(k, 6, mine.at[1, swap], r2b.at[k, 1], {"x": swap}),
        ]
        for copy in s3:
            copy.start()
        for copy in s3:
            copy.wait()
        for h in range(2):
            part[k, core, h, x] = part[k, core, h, x] + r2a[k, h, 0] + r2b[k, h]
        s4 = [move(k, 7 + h, mine.at[h, x, 1 - yhi], r3.at[k, h], over) for h in range(2)]
        for copy in s4:
            copy.start()
        for copy in s4:
            copy.wait()
        for h in range(2):
            total = part[k, core, h, x, yhi] + r3[k, h]
            out_ref[h, k] = total[:, 0:NS]

    for k in range(2):
        all_but_one(got1.at[k, :, pl.ds(0, 47 * 16), :], k, send_sem1, recv_sem1).wait_send()
        all_but_one(got2.at[k, pl.ds(0, 47)], k, send_sem2, recv_sem2).wait_send()


def on_device(columns, freq_blocks, causal_cutoffs, band_index, band_rates):
    inverse, forward = tables()
    vmem = pl.BlockSpec(memory_space=pltpu.VMEM)
    smem = pl.BlockSpec(memory_space=pltpu.SMEM)
    anywhere = pl.BlockSpec(memory_space=pl.ANY)
    dma = pltpu.SemaphoreType.DMA
    return pl.pallas_call(
        kernel,
        out_shape=jax.ShapeDtypeStruct((2, 2, OUT_COLS, NS), F32),
        in_specs=[smem, smem, anywhere, anywhere, vmem, vmem, vmem],
        out_specs=vmem,
        scratch_shapes=[
            pltpu.VMEM((2, 2, NJ, NS), F32),
            pltpu.VMEM((2, 2, NS, CD), F32),
            pltpu.VMEM((NJ, 2 * NSP), BF16),
            pltpu.VMEM((NJ, 2 * NSP), BF16),
            pltpu.VMEM((2, 2 * NSP, 2 * CD), BF16),
            pltpu.VMEM((2, 2 * NSP, 2 * CD), BF16),
            pltpu.VMEM((2, FREQ_DEVICES, 2, 2 * JD, 128), F32),
            pltpu.VMEM((2, 2, NF * JD, 128), F32),
            pltpu.VMEM((JD, TP, CD + 128), F32),
            pltpu.VMEM((JD, TP, CD), BF16),
            pltpu.VMEM((JD, TP, CD), BF16),
            pltpu.VMEM((JD, CD + 128), F32),
            pltpu.VMEM((2, 32, 128), F32),
            pltpu.VMEM((2, 32, 128), F32),
            pltpu.VMEM((2, 2, NF * JD, 128), F32),
            pltpu.VMEM((2, FREQ_DEVICES, 2, 2 * JD, 128), F32),
            pltpu.VMEM((2, CORES, 2, EX, YHI, OUT_COLS, NSP), F32),
            pltpu.VMEM((2, 2, EX, YHI, OUT_COLS, NSP), F32),
            pltpu.VMEM((2, 2, 2, YHI, OUT_COLS, NSP), F32),
            pltpu.VMEM((2, 2, YHI, OUT_COLS, NSP), F32),
            pltpu.VMEM((2, 2, OUT_COLS, NSP), F32),
            dma((4,)),
            dma((4,)),
            dma((2,)),
            dma((2,)),
            dma((2,)),
            dma((2,)),
            dma((2,)),
            dma((2,)),
            dma((2, 9)),
            dma((2, 9)),
        ],
        compiler_params=pltpu.CompilerParams(
            collective_id=0, has_side_effects=True, vmem_limit_bytes=60 * 1024 * 1024
        ),
        name="hessian",
    )(
        causal_cutoffs,
        band_rates,
        columns,
        freq_blocks,
        jnp.broadcast_to(band_index[None, :], (JD, CD)),
        jnp.asarray(inverse),
        jnp.asarray(forward),
    )


def solution(mesh):
    torus = Mesh(mesh.devices.reshape(YLO, ZED, EX, YHI, CORES), AXES)
    freq, cell = ("ylo", "z"), ("x", "yhi", "core")
    placed = (P(None, freq, None, None), P(None, freq, None, cell), P(), P(cell), P())
    return jax.shard_map(
        on_device,
        mesh=torus,
        in_specs=placed,
        out_specs=P(None, freq, cell, None),
        check_vma=False,
    )
```

time: 364 us -> 181 us (0.50)
  waiting for transfers between devices: 206 us -> 0 us
  Pallas kernels: 0 us -> 172 us
  blocking collectives: 53.9 us -> 0 us
  matrix products: 34.3 us -> 0 us
  starting transfers between devices: 31.9 us -> 0 us
  between operations: 13.7 us -> 0.01 us
  local copies, waits for them, and re-layouts: 16 us -> 8.28 us
  other arithmetic: 6.8 us -> 0 us
    pallas_call x0 -> x1, Pallas kernels: none -> 172 us  [on_device(): pl.pallas_call(kernel, out_shape=jax.ShapeDtypeStruct((2, 2, OUT_COLS, NS...]
    reduce_scatter x2 -> x0, waiting for transfers between devices: 140 us -> none  [the longest x1 109 us: summed_rows(): return lax.psum_scatter(parts, chips, scatter_dimension=0, tiled=True)[0]]
    all_to_all x1 -> x0, blocking collectives: 53.9 us -> none  [on_device(): lax.all_to_all(spectrum, 'freq', split_axis=1, concat_axis=2, tiled=True)]
    all_to_all x1 -> x0, waiting for transfers between devices: 51.1 us -> none  [on_device(): lax.all_to_all(local_spectrum, 'freq', split_axis=2, concat_axis=1, tiled...]
    dot_general x10 -> x0, matrix products: 34.3 us -> none  [the longest x1 5.3 us: adjoint_product(): jnp.einsum('kjs,ksm->kjm', columns[1], blocks[0], precision=precise)]
    all_to_all x1 -> x0, starting transfers between devices: 19.7 us -> none  [on_device(): lax.all_to_all(local_spectrum, 'freq', split_axis=2, concat_axis=1, tiled...]
    ppermute x2 -> x0, waiting for transfers between devices: 15.3 us -> none  [the longest x1 12.5 us: extended(): after = lax.ppermute(leading, axis, down)]
    ppermute x2 -> x0, starting transfers between devices: 12.1 us -> none  [the longest x1 10.2 us: extended(): before = lax.ppermute(last, axis, up)]
  transfers between devices with their start and end apart: 5 -> 0, of which waited for: 5 -> 0; matrix products, arithmetic and copies ran while one was open for 0% -> 0% of each run, Pallas kernels for 0% -> 0%
where the time goes in v1:
time: 181 us
  Pallas kernels  172 us (95%)
  local copies, waits for them, and re-layouts  8.28 us (5%)
    pallas_call x1, Pallas kernels, on_device(): pl.pallas_call(kernel, out_shape=jax.ShapeDtypeStruct((2, 2, OUT_COLS, NS...  172 us
    unnamed x2, local copies, waits for them, and re-layouts  7 us

profile of v1, /device:TPU:1, one launch (start us, length us, event | category | flops | bytes accessed | tf_op | source)
XLA Modules:
  0.0 180.8 jit_solution(18302941524379534460)
XLA Ops:
  0.0 1.3 broadcast_in_dim.2.bands_ref
  1.3 5.3 %copy.8.cols_ref = f32[2,2,384,600]{3,2,1,0:T(8,128)} copy(f32[2,2,384,600]{2,3,1,0:T(8,128)} %param.7) | data formatting | bytes 7372800 | tf_op args[0]
  6.6 172.5 %hessian.1 = f32[2,2,24,600]{3,2,1,0:T(8,128)} custom-call(s32[384]{0:T(512)} %cut_ref.1, f32[8]{0:T(128)} %rates_ref.1, f32[2,2,384,600]{3,2,1,0:T(8,128)} %copy.8.cols_ref, f32[2,2,600,256]{3,2,1,0:T(8,128)} %blocks_ref.1, s32[8,256]{1,0:T(8,128)} %broadcast_in_dim.2.bands_ref, bf16[192,192]{1,0:T(8,128)(2,1)} %constant.4.clone.inv_ref, ...), custom_call_target="tpu_custom_call" | custom-call | tf_op jit(solution)/shard_map/hessian/pallas_call | solution.py:350
  179.1 1.7 copy.10

commit v2 on v1

v2 whole, which is shorter than its diff:
```python
import math

import jax
import jax.numpy as jnp
import numpy as np
from jax import lax
from jax.experimental import pallas as pl
from jax.experimental.pallas import tpu as pltpu
from jax.sharding import Mesh
from jax.sharding import PartitionSpec as P

AXES = ("ylo", "z", "x", "yhi", "core")
YLO, ZED, EX, YHI, CORES = 4, 12, 4, 2, 2
FREQ_DEVICES = YLO * ZED
NF = 96
NT = 95
TP = 96
NS = 600
NSP = 640
NJ = 384
JD = 8
CD = 256
SWEEPS = 4
BANDS = 8
OUT_COLS = 24
MESH = pl.DeviceIdType.MESH
F32, BF16 = jnp.float32, jnp.bfloat16


def halves(table):
    high = table.astype(np.float32).astype(jnp.bfloat16)
    low = (table - high.astype(np.float64)).astype(jnp.bfloat16)
    return high, low


def tables():
    cycle = 2 * NT
    k = np.arange(NF)
    t = np.arange(NT)
    angle = 2.0 * math.pi * ((t[:, None] * k[None, :]) % cycle) / cycle
    weight = np.where((k == 0) | (k == NF - 1), 1.0, 2.0) / cycle
    inv = np.stack([weight * np.cos(angle), -weight * np.sin(angle)], axis=-1)
    inv = inv.reshape(NT, FREQ_DEVICES, 2, 2).transpose(0, 2, 1, 3).reshape(NT, 2 * NF)
    inv = np.concatenate([inv, np.zeros((TP - NT, 2 * NF))], axis=0)
    fwd = np.stack([np.cos(angle), -np.sin(angle)], axis=-1)
    fwd = fwd.reshape(NT, FREQ_DEVICES, 2, 2).transpose(2, 1, 3, 0).reshape(2, NF, NT)
    fwd = np.concatenate([fwd, np.zeros((2, NF, TP - NT))], axis=2)
    return (
        np.concatenate(halves(inv), axis=0),
        np.concatenate(halves(fwd), axis=1),
    )


def split(x):
    high = x.astype(BF16)
    return high, (x - high.astype(F32)).astype(BF16)


def mm(a, b):
    return lax.dot_general(a, b, (((1,), (0,)), ((), ())), preferred_element_type=F32)


def mt(a, b):
    return lax.dot_general(a, b, (((1,), (1,)), ((), ())), preferred_element_type=F32)


def kernel(
    cut_ref, rates_ref, cols_ref, blocks_ref, bands_ref, inv_ref, fwd_ref, out_ref,
    cols, blocks, vh, vl, gh, gl, adj, got1, ext, uh, ul, rate, pack, halo, send2, got2,
    part, r1, r2, r3,
    load_sem, self_sem, ssem1, rsem1, ssem2, rsem2, hsend, hrecv, rsend, rrecv,
):
    y, z = lax.axis_index("ylo"), lax.axis_index("z")
    x, yhi, core = lax.axis_index("x"), lax.axis_index("yhi"), lax.axis_index("core")
    me = y * ZED + z
    cell = (x * YHI + yhi) * CORES + core

    loads = []
    for k in range(2):
        loads.append(pltpu.make_async_copy(cols_ref.at[:, k], cols.at[k], load_sem.at[2 * k]))
        loads.append(pltpu.make_async_copy(blocks_ref.at[:, k], blocks.at[k], load_sem.at[2 * k + 1]))
    for copy in loads:
        copy.start()

    rows_of_peers = [lax.rem(y + 3 - turn, YLO) for turn in range(4)]

    def for_peers(act):
        def some(step, count):
            half = 5 - lax.div(step - 1, 2)
            dz = jnp.where(lax.rem(step, 2) == 1, half, 12 - half)
            dz = jnp.where(step == 0, 6, jnp.where(step == 11, 0, dz))
            pz = lax.rem(z + dz, ZED)
            for py in rows_of_peers[:count]:
                act(py, pz)

        def body(step, carry):
            some(step, 4)
            return carry

        lax.fori_loop(0, 11, body, 0)
        some(jnp.int32(11), 3)

    def cell_peer(c):
        c = lax.rem(c + 16, 16)
        return {"x": lax.div(c, 4), "yhi": lax.rem(lax.div(c, 2), 2), "core": lax.rem(c, 2)}

    left, right = cell_peer(cell - 1), cell_peer(cell + 1)
    sibling, over = {"core": 1 - core}, {"yhi": 1 - yhi}
    across = [{"x": lax.rem(x + d, EX)} for d in (1, 2, 3)]

    barrier = pltpu.get_barrier_semaphore()

    def greet(py, pz):
        pl.semaphore_signal(barrier, inc=1, device_id={"ylo": py, "z": pz}, device_id_type=MESH)

    for_peers(greet)
    friends = [left, right, sibling, over, *across]
    for friend in friends:
        pl.semaphore_signal(barrier, inc=1, device_id=friend, device_id_type=MESH)

    def remote(source, target, send_sem, recv_sem, friend):
        return pltpu.make_async_remote_copy(
            src_ref=source,
            dst_ref=target,
            send_sem=send_sem,
            recv_sem=recv_sem,
            device_id=friend,
            device_id_type=MESH,
        )

    def rows8(f):
        return pl.ds(pl.multiple_of(8 * f, 8), 8)

    def exchange(source, target, send_sem, recv_sem):
        def send(py, pz):
            friend = {"ylo": py, "z": pz}
            remote(source(py * ZED + pz), target(me), send_sem, recv_sem, friend).start()

        for_peers(send)

    def arrived(buffer, sem):
        remote(buffer, buffer, sem, sem, sibling).wait_recv()

    def left_here(buffer, sem):
        remote(buffer, buffer, sem, sem, sibling).wait_send()

    top8 = lax.broadcasted_iota(jnp.int32, (1, JD, 128), 1) < 4

    def operands(k):
        for p in range(2):
            value = jnp.concatenate([cols[k, p], jnp.zeros((NSP - NS, NJ), F32)], axis=0)
            high, low = split(value.T)
            vh[:, p * NSP : p * NSP + NSP] = high
            vl[:, p * NSP : p * NSP + NSP] = low
        for p in range(2):
            value = jnp.concatenate([blocks[k, p], jnp.zeros((NSP - NS, CD), F32)], axis=0)
            high, low = split(value)
            for into, half in ((gh, high), (gl, low)):
                if p == 0:
                    into[k, 0:NSP, 0:CD] = half
                    into[k, NSP:, CD:] = half
                else:
                    into[k, 0:NSP, CD:] = -half
                    into[k, NSP:, 0:CD] = half

    own1, own2 = [], []
    for k in range(2):
        loads[2 * k].wait()
        loads[2 * k + 1].wait()
        operands(k)
        both = mm(vh[...], gh[k]) + mm(vh[...], gl[k]) + mm(vl[...], gh[k])
        for h in range(2):
            real = both[:, h * 128 : h * 128 + 128].reshape(FREQ_DEVICES, JD, 128)
            imag = both[:, CD + h * 128 : CD + h * 128 + 128].reshape(FREQ_DEVICES, JD, 128)
            adj[0, :, k, h] = jnp.where(top8, real, pltpu.roll(imag, 4, 1))
            adj[1, :, k, h] = jnp.where(top8, pltpu.roll(real, 4, 1), imag)
        if k == 0:
            pl.semaphore_wait(barrier, FREQ_DEVICES - 1 + len(friends))
        exchange(
            lambda f: adj.at[0, f, k], lambda f: got1.at[0, k, :, rows8(f), :], ssem1.at[0], rsem1.at[0]
        )
    exchange(lambda f: adj.at[1, f], lambda f: got1.at[1, :, :, rows8(f), :], ssem1.at[1], rsem1.at[1])
    for a in range(2):
        own1.append(
            pltpu.make_async_copy(adj.at[a, me], got1.at[a, :, :, rows8(me), :], self_sem.at[a])
        )
        own1[a].start()

    band = jnp.broadcast_to(bands_ref[...], (JD, CD))
    own_rate = jnp.zeros((JD, CD), F32)
    for b in range(BANDS):
        own_rate = own_rate + jnp.where(band == b, rates_ref[b], 0.0)
    rate[:, 0:CD] = own_rate

    time = lax.broadcasted_iota(jnp.int32, (TP, CD), 0)
    lane = lax.broadcasted_iota(jnp.int32, (TP // 4, 128), 1)
    lane8 = lax.broadcasted_iota(jnp.int32, (JD, 128), 1)
    after = jnp.where(cell < 15, 1.0, 0.0)
    before = jnp.where(cell > 0, 1.0, 0.0)

    def middle(a):
        own1[a].wait()
        arrived(got1.at[a, :, :, pl.ds(0, 47 * 8), :], rsem1.at[a])
        to_left = jnp.zeros((TP // 4, 128), F32)
        to_right = jnp.zeros((TP // 4, 128), F32)
        for j in range(4):
            value = jnp.concatenate(
                [
                    jnp.concatenate(
                        [got1[a, k, h, pl.ds(j, NF, stride=4), :] for h in range(2)], axis=1
                    )
                    for k in range(2)
                ],
                axis=0,
            )
            high, low = split(value)
            main = mm(inv_ref[...], high)
            series = main[0:TP] + main[TP:] + mm(inv_ref[0:TP], low)
            series = jnp.where(time < cut_ref[JD * me + 4 * a + j], series, 0.0)
            ext[a, j, :, 0:CD] = series
            for g in range(4):
                rows = slice(g * 24, g * 24 + 24)
                at = 32 * g + 4 * j
                here = (lane >= at) & (lane < at + 4)
                head, tail = series[rows, 0:128], series[rows, 128:256]
                head = pltpu.roll(head, at, 1) if at else head
                tail = pltpu.roll(tail, at + 4, 1)
                to_left = jnp.where(here, head, to_left)
                to_right = jnp.where(here, tail, to_right)
        pack[a, 0, 0:24] = to_left
        pack[a, 1, 0:24] = to_right
        pack[a, 0, 24:32] = rate[:, 0:128]
        pack[a, 1, 24:32] = rate[:, 128:256]
        edge = [
            remote(pack.at[a, side], halo.at[a, side], hsend.at[a, side], hrecv.at[a, side], friend)
            for side, friend in ((0, left), (1, right))
        ]
        for copy in edge:
            copy.start()
        for copy in edge:
            copy.wait()

        from_right, from_left = halo[a, 0, 0:24] * after, halo[a, 1, 0:24] * before
        far = jnp.where(lane8 < 4, halo[a, 0, 24:32] * after, 0.0)
        far = jnp.where(lane8 >= 124, halo[a, 1, 24:32] * before, far)
        rate[:, CD:] = far
        for j in range(4):
            for g in range(4):
                at = 32 * g + 4 * j
                first = pltpu.roll(from_right, 128 - at, 1) if at else from_right
                last = pltpu.roll(from_left, (252 - at) % 128, 1)
                tile = jnp.where(lane < 4, first, jnp.where(lane >= 124, last, 0.0))
                ext[a, j, g * 24 : g * 24 + 24, CD:] = tile

        def smooth(j, carry):
            field = ext[a, j]
            rates = rate[0:1, :]
            for _ in range(SWEEPS):
                field = field + rates * (
                    pltpu.roll(field, 1, 1) - 2.0 * field + pltpu.roll(field, CD + 127, 1)
                )
            high, low = split(field[:, 0:CD])
            uh[4 * a + j] = high
            ul[4 * a + j] = low
            return carry

        lax.fori_loop(0, 4, smooth, 0)

        for k in range(2):
            for j in range(4):
                main = mm(fwd_ref[k], uh[4 * a + j])
                main = main[0:NF] + main[NF:] + mm(fwd_ref[k, 0:NF], ul[4 * a + j])
                for h in range(2):
                    send2[a, k, h, pl.ds(j, NF, stride=4), :] = main[:, h * 128 : h * 128 + 128]
            if a == 1:
                exchange(
                    lambda f: send2.at[1, k, :, rows8(f), :],
                    lambda f: got2.at[1, f, k],
                    ssem2.at[1 + k],
                    rsem2.at[1 + k],
                )
        if a == 0:
            exchange(
                lambda f: send2.at[0, :, :, rows8(f), :], lambda f: got2.at[0, f], ssem2.at[0], rsem2.at[0]
            )
        own2.append(
            pltpu.make_async_copy(send2.at[a, :, :, rows8(me), :], got2.at[a, me], self_sem.at[2 + a])
        )
        own2[a].start()

    class Unit:
        def __init__(self, index, a, k, low, high):
            self.a, self.k, self.u = a, k, 2 * a + k
            self.low, self.high = low, high
            lanes = pl.ds(low, high - low)
            whole, u = part.at[self.u], self.u
            self.first = [
                remote(
                    whole.at[1 - core, :, :, :, lanes], r1.at[u, :, :, :, lanes],
                    rsend.at[index, 0], rrecv.at[index, 0], sibling,
                )
            ]
            self.second = [
                remote(
                    whole.at[core, lax.rem(x + d + 1, EX), :, :, lanes], r2.at[u, d, :, :, lanes],
                    rsend.at[index, 1 + d], rrecv.at[index, 1 + d], across[d],
                )
                for d in (1, 0, 2)
            ]
            self.third = [
                remote(
                    whole.at[core, x, 1 - yhi, :, lanes], r3.at[u, :, lanes],
                    rsend.at[index, 4], rrecv.at[index, 4], over,
                )
            ]

        def multiply(self):
            a, k = self.a, self.k
            low, high = self.low, self.high
            quarters = [split(got2[a, :, k, h].reshape(NJ, 128)) for h in range(2)]
            ch = jnp.concatenate([q[0] for q in quarters], axis=1)
            cl = jnp.concatenate([q[1] for q in quarters], axis=1)

            def product(start):
                rows = slice(start + low, start + high)
                gr, gs = gh[k, rows, 0:CD], gl[k, rows, 0:CD]
                return mt(ch, gr) + mt(ch, gs) + mt(cl, gr)

            width = high - low
            plain = product(0).reshape(FREQ_DEVICES, JD, width)
            cross = pltpu.roll(product(NSP).reshape(FREQ_DEVICES, JD, width), 4, 1)
            top = lax.broadcasted_iota(jnp.int32, (1, JD, width), 1) < 4
            total = (plain + jnp.where(top, -cross, cross)).reshape(NJ, width)
            for c in range(16):
                part[self.u, c % 2, c // 4, (c // 2) % 2, :, low:high] = total[
                    c * OUT_COLS : (c + 1) * OUT_COLS
                ]
            for copy in self.first:
                copy.start()

        def after_first(self):
            lanes, u = slice(self.low, self.high), self.u
            for copy in self.first:
                copy.wait()
            part[u, core, :, :, :, lanes] = part[u, core, :, :, :, lanes] + r1[u, :, :, :, lanes]
            for copy in self.second:
                copy.start()

        def after_second(self):
            lanes, u = slice(self.low, self.high), self.u
            for copy in self.second:
                copy.wait()
            total = part[u, core, x, :, :, lanes]
            for d in range(3):
                total = total + r2[u, d, :, :, lanes]
            part[u, core, x, :, :, lanes] = total
            for copy in self.third:
                copy.start()

        def after_third(self):
            lanes, u = slice(self.low, self.high), self.u
            for copy in self.third:
                copy.wait()
            r3[u, :, lanes] = part[u, core, x, yhi, :, lanes] + r3[u, :, lanes]

    middle(0)
    middle(1)

    own2[0].wait()
    arrived(got2.at[0, pl.ds(0, 47)], rsem2.at[0])
    ua, ub, uc = Unit(0, 0, 0, 0, NSP), Unit(1, 0, 1, 0, NSP), Unit(2, 1, 0, 0, NSP)
    ud, ue = Unit(3, 1, 1, 0, 384), Unit(4, 1, 1, 384, NSP)
    ua.multiply()
    ub.multiply()
    ua.after_first()
    ub.after_first()
    ua.after_second()
    own2[1].wait()
    arrived(got2.at[1, pl.ds(0, 47), 0], rsem2.at[1])
    uc.multiply()
    ub.after_second()
    uc.after_first()
    ua.after_third()
    uc.after_second()
    arrived(got2.at[1, pl.ds(0, 47), 1], rsem2.at[2])
    ud.multiply()
    ue.multiply()
    ub.after_third()
    ud.after_first()
    ue.after_first()
    ud.after_second()
    ue.after_second()
    uc.after_third()
    ud.after_third()
    ue.after_third()

    top = lax.broadcasted_iota(jnp.int32, (JD, NS), 0) < 4
    for k in range(2):
        for t in range(3):
            rows = slice(8 * t, 8 * t + 8)
            first, last = r3[k, rows, 0:NS], r3[2 + k, rows, 0:NS]
            out_ref[0, k, rows] = jnp.where(top, first, pltpu.roll(last, 4, 0))
            out_ref[1, k, rows] = jnp.where(top, pltpu.roll(first, 4, 0), last)

    for a in range(2):
        left_here(got1.at[a, :, :, pl.ds(0, 47 * 8), :], ssem1.at[a])
    left_here(got2.at[0, pl.ds(0, 47)], ssem2.at[0])
    for k in range(2):
        left_here(got2.at[1, pl.ds(0, 47), k], ssem2.at[1 + k])


def on_device(columns, freq_blocks, causal_cutoffs, band_index, band_rates):
    inverse, forward = tables()
    vmem = pl.BlockSpec(memory_space=pltpu.VMEM)
    smem = pl.BlockSpec(memory_space=pltpu.SMEM)
    anywhere = pl.BlockSpec(memory_space=pl.ANY)
    dma = pltpu.SemaphoreType.DMA
    return pl.pallas_call(
        kernel,
        out_shape=jax.ShapeDtypeStruct((2, 2, OUT_COLS, NS), F32),
        in_specs=[smem, smem, anywhere, anywhere, vmem, vmem, vmem],
        out_specs=vmem,
        scratch_shapes=[
            pltpu.VMEM((2, 2, NS, NJ), F32),
            pltpu.VMEM((2, 2, NS, CD), F32),
            pltpu.VMEM((NJ, 2 * NSP), BF16),
            pltpu.VMEM((NJ, 2 * NSP), BF16),
            pltpu.VMEM((2, 2 * NSP, 2 * CD), BF16),
            pltpu.VMEM((2, 2 * NSP, 2 * CD), BF16),
            pltpu.VMEM((2, FREQ_DEVICES, 2, 2, JD, 128), F32),
            pltpu.VMEM((2, 2, 2, NF * 4, 128), F32),
            pltpu.VMEM((2, 4, TP, CD + 128), F32),
            pltpu.VMEM((JD, TP, CD), BF16),
            pltpu.VMEM((JD, TP, CD), BF16),
            pltpu.VMEM((JD, CD + 128), F32),
            pltpu.VMEM((2, 2, 32, 128), F32),
            pltpu.VMEM((2, 2, 32, 128), F32),
            pltpu.VMEM((2, 2, 2, NF * 4, 128), F32),
            pltpu.VMEM((2, FREQ_DEVICES, 2, 2, JD, 128), F32),
            pltpu.VMEM((4, CORES, EX, YHI, OUT_COLS, NSP), F32),
            pltpu.VMEM((4, EX, YHI, OUT_COLS, NSP), F32),
            pltpu.VMEM((4, 3, YHI, OUT_COLS, NSP), F32),
            pltpu.VMEM((4, OUT_COLS, NSP), F32),
            dma((4,)),
            dma((4,)),
            dma((2,)),
            dma((2,)),
            dma((3,)),
            dma((3,)),
            dma((2, 2)),
            dma((2, 2)),
            dma((5, 5)),
            dma((5, 5)),
        ],
        compiler_params=pltpu.CompilerParams(
            collective_id=0, has_side_effects=True, vmem_limit_bytes=60 * 1024 * 1024
        ),
        name="hessian",
    )(
        causal_cutoffs,
        band_rates,
        jnp.swapaxes(columns, 2, 3),
        freq_blocks,
        band_index.reshape(1, CD),
        jnp.asarray(inverse),
        jnp.asarray(forward),
    )


def solution(mesh):
    torus = Mesh(mesh.devices.reshape(YLO, ZED, EX, YHI, CORES), AXES)
    freq, cell = ("ylo", "z"), ("x", "yhi", "core")
    placed = (P(None, freq, None, None), P(None, freq, None, cell), P(), P(cell), P())
    return jax.shard_map(
        on_device,
        mesh=torus,
        in_specs=placed,
        out_specs=P(None, freq, cell, None),
        check_vma=False,
    )
```

time: 181 us -> 146 us (0.81)
  Pallas kernels: 172 us -> 144 us
  local copies, waits for them, and re-layouts: 8.28 us -> 1.65 us
    pallas_call x1, Pallas kernels: 172 us -> 144 us  [on_device(): pl.pallas_call(kernel, out_shape=jax.ShapeDtypeStruct((2, 2, OUT_COLS, NS...]
    unnamed x2 -> x1, local copies, waits for them, and re-layouts: 7 us -> 1.65 us
where the time goes in v2:
time: 146 us; the launch traced here: 145 us
  Pallas kernels  144 us (99%)
  local copies, waits for them, and re-layouts  1.65 us (1%)
    pallas_call x1, Pallas kernels, on_device(): pl.pallas_call(kernel, out_shape=jax.ShapeDtypeStruct((2, 2, OUT_COLS, NS...  144 us

profile of v2, /device:TPU:1, one launch (start us, length us, event | category | flops | bytes accessed | tf_op | source)
XLA Modules:
  0.0 145.4 jit_solution(16103031381013904377)
XLA Ops:
  0.0 143.8 %hessian.1 = f32[2,2,24,600]{3,2,1,0:T(8,128)} custom-call(s32[384]{0:T(512)} %cut_ref.1, f32[8]{0:T(128)} %rates_ref.1, f32[2,2,600,384]{3,2,1,0:T(8,128)} %bitcast.2, f32[2,2,600,256]{3,2,1,0:T(8,128)} %blocks_ref.1, s32[1,256]{1,0:T(1,128)} %bitcast.3, bf16[192,192]{1,0:T(8,128)(2,1)} %constant.4.clone.inv_ref, bf16[2,192,96]{2,1,0:T(8,128)(2,1)} %constant.5.clone.fwd_ref), custom_call_target="tpu_custom_call" | custom-call | tf_op jit(solution)/shard_map/hessian/pallas_call | solution.py:418
  143.8 1.7 %copy.9 = f32[2,2,24,600]{3,2,1,0:T(8,128)} copy(f32[2,2,24,600]{3,2,1,0:T(8,128)} %hessian.1) | data formatting | bytes 460800

commit v3 on v2

--- a/solution.py
+++ b/solution.py
@@ -79,7 +79,7 @@
     for k in range(2):
         loads.append(pltpu.make_async_copy(cols_ref.at[:, k], cols.at[k], load_sem.at[2 * k]))
         loads.append(pltpu.make_async_copy(blocks_ref.at[:, k], blocks.at[k], load_sem.at[2 * k + 1]))
-    for copy in loads:
+    for copy in loads[0:2]:
         copy.start()
 
     rows_of_peers = [lax.rem(y + 3 - turn, YLO) for turn in range(4)]
@@ -167,6 +167,9 @@
     for k in range(2):
         loads[2 * k].wait()
         loads[2 * k + 1].wait()
+        if k == 0:
+            for copy in loads[2:4]:
+                copy.start()
         operands(k)
         both = mm(vh[...], gh[k]) + mm(vh[...], gl[k]) + mm(vl[...], gh[k])
         for h in range(2):
@@ -369,7 +372,7 @@
     own2[0].wait()
     arrived(got2.at[0, pl.ds(0, 47)], rsem2.at[0])
     ua, ub, uc = Unit(0, 0, 0, 0, NSP), Unit(1, 0, 1, 0, NSP), Unit(2, 1, 0, 0, NSP)
-    ud, ue = Unit(3, 1, 1, 0, 384), Unit(4, 1, 1, 384, NSP)
+    ud, ue, uf = Unit(3, 1, 1, 0, 256), Unit(4, 1, 1, 256, 512), Unit(5, 1, 1, 512, NSP)
     ua.multiply()
     ub.multiply()
     ua.after_first()
@@ -381,18 +384,22 @@
     ub.after_second()
     uc.after_first()
     ua.after_third()
-    uc.after_second()
     arrived(got2.at[1, pl.ds(0, 47), 1], rsem2.at[2])
     ud.multiply()
     ue.multiply()
+    ud.after_first()
+    uf.multiply()
+    ue.after_first()
+    uf.after_first()
+    uc.after_second()
     ub.after_third()
-    ud.after_first()
-    ue.after_first()
     ud.after_second()
     ue.after_second()
+    uf.after_second()
     uc.after_third()
     ud.after_third()
     ue.after_third()
+    uf.after_third()
 
     top = lax.broadcasted_iota(jnp.int32, (JD, NS), 0) < 4
     for k in range(2):
@@ -449,8 +456,8 @@
             dma((3,)),
             dma((2, 2)),
             dma((2, 2)),
-            dma((5, 5)),
-            dma((5, 5)),
+            dma((6, 5)),
+            dma((6, 5)),
         ],
         compiler_params=pltpu.CompilerParams(
             collective_id=0, has_side_effects=True, vmem_limit_bytes=60 * 1024 * 1024

time: 146 us -> 143 us (0.979)
  Pallas kernels: 144 us -> 142 us
    pallas_call x1, Pallas kernels: 144 us -> 142 us  [on_device(): pl.pallas_call(kernel, out_shape=jax.ShapeDtypeStruct((2, 2, OUT_COLS, NS...]
where the time goes in v3:
time: 143 us
  Pallas kernels  142 us (99%)
  local copies, waits for them, and re-layouts  1.65 us (1%)
    pallas_call x1, Pallas kernels, on_device(): pl.pallas_call(kernel, out_shape=jax.ShapeDtypeStruct((2, 2, OUT_COLS, NS...  142 us

profile of v3, /device:TPU:1, one launch (start us, length us, event | category | flops | bytes accessed | tf_op | source)
XLA Modules:
  0.0 143.2 jit_solution(14073883705909400881)
XLA Ops:
  0.0 141.5 %hessian.1 = f32[2,2,24,600]{3,2,1,0:T(8,128)} custom-call(s32[384]{0:T(512)} %cut_ref.1, f32[8]{0:T(128)} %rates_ref.1, f32[2,2,600,384]{3,2,1,0:T(8,128)} %bitcast.2, f32[2,2,600,256]{3,2,1,0:T(8,128)} %blocks_ref.1, s32[1,256]{1,0:T(1,128)} %bitcast.3, bf16[192,192]{1,0:T(8,128)(2,1)} %constant.4.clone.inv_ref, bf16[2,192,96]{2,1,0:T(8,128)(2,1)} %constant.5.clone.fwd_ref), custom_call_target="tpu_custom_call" | custom-call | tf_op jit(solution)/shard_map/hessian/pallas_call | solution.py:425
  141.5 1.7 %copy.9 = f32[2,2,24,600]{3,2,1,0:T(8,128)} copy(f32[2,2,24,600]{3,2,1,0:T(8,128)} %hessian.1) | data formatting | bytes 460800
